TPU v7x, 32 devices: a whole 2x2x4 slice. The times are simulated.
32 devices in a mesh: node: 8 (over z, y), local: 4 (over x, core).
Axes of the slice: x: 2, y: 2, z: 4, core: 2. Of those that a mesh axis runs over, the one named last changes fastest.
Arguments:
- tokens: bfloat16 [4096, 7168], P(('node', 'local')), may hold values from -6 to 6
- w_gate: bfloat16 [8, 7168, 1024], P('node', None, 'local'), may hold values from -0.0625 to 0.0625
- w_up: bfloat16 [8, 7168, 1024], P('node', None, 'local'), may hold values from -0.0625 to 0.0625
- w_down: bfloat16 [8, 1024, 7168], P('node', 'local'), may hold values from -0.1875 to 0.1875
- chosen: int32 [8, 48], replicated, may hold values from 0 to 4095, as said below
- counts: int32 [8], replicated, may hold values from 3 to 48, as said below
- gates: float32 [8, 48], replicated, may hold values from 0.2 to 1
Outputs:
- mixed: bfloat16 [4096, 7168], P(('node', 'local'))
Inputs may be any that keep to these rules, and one draw needn't show every extreme that they name: `chosen`: each expert's list holds distinct tokens; in each list at most 3 entries lie in one device's block of 128 consecutive tokens, and for every expert some block holds exactly 3 live entries. `counts`: some expert has exactly 48 live entries.
All inputs are finite; a program needn't handle non-finite values.
Results may differ from a plain program's by a relative error of at most 0.014.
Values may be sent and summed in bfloat16 or wider, within the bound.
A program may use at most 128 MiB of HBM per device.

v0:
```python
import functools

import jax
import jax.numpy as jnp
from jax import lax
from jax.experimental import pallas as pl
from jax.experimental.pallas import tpu as pltpu
from jax.sharding import PartitionSpec as P

SLOT = 3
SUB, LANE = 8, 128
COLS = SUB * LANE
MESH = pl.DeviceIdType.MESH
DISPATCH_GROUPS = 1
COMBINE_GROUPS = 4


def split(count, groups):
    groups = min(groups, count)
    sizes = [count // groups + (1 if g < count % groups else 0) for g in range(groups)]
    starts = [sum(sizes[:g]) for g in range(groups)]
    return list(zip(starts, sizes))


def kernel(dims, counts_hbm, chosen_hbm, gates_hbm, tokens_hbm, wg_hbm, wu_hbm, wd_hbm, out_ref, place_ref,
           counts_ref, chosen_ref, gates_ref, tokens_ref, wg, wu, wd, tx, rx, py, r1b, s2, r2b, a3, ax, stage,
           wsem, lsem, bsem, d1s, d1r, d2s, d2r, d3s, d3r, d4s, d4r, r1s, r1r, r2s, r2r, r3s, r3r):
    n_node, n_local, chunks, tok_dev, ff = dims
    nx = n_local // 2
    experts, cap = chosen_ref.shape
    per = n_node * SLOT
    rows = n_local * per
    padded = out_ref.shape[0] // 2
    f32, bf16 = jnp.float32, jnp.bfloat16
    me_n, me_l = lax.axis_index("node"), lax.axis_index("local")
    me_x, me_c = me_l // 2, me_l % 2
    partner = me_x * 2 + (1 - me_c)
    dgroups, cgroups = split(chunks, DISPATCH_GROUPS), split(chunks, COMBINE_GROUPS)

    paired = n_node & (n_node - 1) == 0

    def node_at(k):
        if paired:
            return jnp.bitwise_xor(me_n, abs(k))
        return lax.rem(me_n + k + n_node, n_node)

    def x_at(k):
        return lax.rem(me_x + k + nx, nx)

    def remote(src, dst, ssem, rsem, node, local):
        return pltpu.make_async_remote_copy(
            src_ref=src, dst_ref=dst, send_sem=ssem, recv_sem=rsem,
            device_id=(node, local), device_id_type=MESH)

    sent = []

    def send(*args):
        copy = remote(*args)
        copy.start()
        sent.append(copy)

    barrier = pltpu.get_barrier_semaphore()
    for k in range(1, n_node):
        pl.semaphore_signal(barrier, inc=1, device_id=(node_at(k), me_l), device_id_type=MESH)
    pl.semaphore_signal(barrier, inc=1, device_id=(me_n, partner), device_id_type=MESH)
    for k in range(1, nx):
        pl.semaphore_signal(barrier, inc=1, device_id=(me_n, x_at(k) * 2 + me_c), device_id_type=MESH)

    loads = [pltpu.make_async_copy(src, dst, wsem.at[i]) for i, (src, dst) in enumerate((
        (wg_hbm.at[0], wg), (wu_hbm.at[0], wu), (wd_hbm.at[0], wd), (tokens_hbm, tokens_ref),
        (counts_hbm, counts_ref), (chosen_hbm, chosen_ref), (gates_hbm, gates_ref)))]
    for copy in loads[4:] + [loads[3]] + loads[:3]:
        copy.start()
    for copy in loads[4:]:
        copy.wait()

    base = (me_n * n_local + me_l) * tok_dev
    row = lax.broadcasted_iota(jnp.int32, (experts, cap), 0)
    count = jnp.zeros((experts, cap), jnp.int32)
    for e in range(experts):
        count = jnp.where(row == e, counts_ref[e], count)
    pos = chosen_ref[...] - base
    mine = (lax.broadcasted_iota(jnp.int32, (experts, cap), 1) < count) & (pos >= 0) & (pos < tok_dev)
    before = (lax.broadcasted_iota(jnp.int32, (cap, cap), 0)
              < lax.broadcasted_iota(jnp.int32, (cap, cap), 1))
    rank = jnp.dot(jnp.where(mine, 1.0, 0.0).astype(bf16), jnp.where(before, 1.0, 0.0).astype(bf16),
                   preferred_element_type=f32)
    pos1 = (pos + 1).astype(f32)
    lane1 = (lax.broadcasted_iota(jnp.int32, (experts, tok_dev), 1) + 1).astype(f32)
    picks, weights = [], []
    for s in range(SLOT):
        sel = mine & (rank == float(s))
        where = jnp.sum(jnp.where(sel, pos1, 0.0), axis=1, keepdims=True)
        gate = jnp.sum(jnp.where(sel, gates_ref[...], 0.0), axis=1, keepdims=True)
        hit = lane1 == where
        picks.append(jnp.where(hit, 1.0, 0.0))
        weights.append(jnp.where(hit, gate, 0.0))
    pick = jnp.concatenate(picks, axis=0)
    weight = jnp.concatenate(weights, axis=0)
    col = lax.broadcasted_iota(jnp.int32, (per, per), 1)
    slot = jnp.zeros((per, per), jnp.int32)
    for s in range(1, SLOT):
        slot = slot + jnp.where(col >= s * experts, 1, 0)
    order = lax.broadcasted_iota(jnp.int32, (per, per), 0) == (col - slot * experts) * SLOT + slot
    order = jnp.where(order, 1.0, 0.0).astype(bf16)
    high = weight.astype(bf16)
    low = (weight - high.astype(f32)).astype(bf16)

    def ordered(x):
        return jnp.dot(order, x, preferred_element_type=f32)

    select = ordered(pick.astype(bf16)).astype(bf16)
    fill = jnp.zeros((padded - per, tok_dev), f32)
    parts = [ordered(high), fill, ordered(low), fill] if padded > per else [ordered(high), ordered(low)]
    place_ref[...] = jnp.transpose(jnp.concatenate(parts, axis=0)).astype(bf16)
    if padded > per:
        out_ref[...] = jnp.zeros_like(out_ref)

    def to_tiles(value, m):
        for q in range(SUB):
            stage[pl.ds(q, m, stride=SUB), :] = value[:, q * LANE:(q + 1) * LANE]
        return stage[pl.ds(0, m * SUB), :].astype(bf16).reshape(m, SUB, LANE)

    def from_tiles(value, m):
        stage[pl.ds(0, m * SUB), :] = value.reshape(m * SUB, LANE).astype(f32)
        return jnp.concatenate(
            [stage[pl.ds(q, m, stride=SUB), :].astype(bf16) for q in range(SUB)], axis=1)

    mine_rows = pl.ds(me_n * SLOT, SLOT)
    near_first = list(range(n_node))
    far_first = near_first[:0:-1]
    own = []
    loads[3].wait()
    for g, (j0, jn) in enumerate(dgroups):
        js = pl.ds(j0, jn)
        for j in range(j0, j0 + jn):
            picked = jnp.dot(select, tokens_ref[:, j * COLS:(j + 1) * COLS], preferred_element_type=f32)
            tx[j] = to_tiles(picked, per)
        if g == 0:
            pl.semaphore_wait(barrier, n_node - 1 + 1 + nx - 1)
        for k in near_first[1:]:
            dst = node_at(k)
            send(tx.at[js, pl.ds(dst * SLOT, SLOT)], rx.at[js, me_l, mine_rows],
                 d1s.at[g, k], d1r.at[g, k], dst, me_l)
        copy = pltpu.make_async_copy(tx.at[js, mine_rows], rx.at[js, me_l, mine_rows], lsem.at[g])
        copy.start()
        own.append(copy)


    def block(js, local, node):
        return rx.at[js, local, pl.ds(node * SLOT, SLOT)]

    def pass_on(g):
        j0, jn = dgroups[g]
        js = pl.ds(j0, jn)
        for k in near_first:
            src = node_at(-k)
            here = block(js, me_l, src)
            if k == 0:
                out = tx.at[js, mine_rows]
            else:
                remote(here, here, d1s.at[g, k], d1r.at[g, k], me_n, partner).wait_recv()
                out = here
            for d in range(1, nx):
                send(out, here, d2s.at[g, k, d], d2r.at[g, k, d], me_n, x_at(d) * 2 + me_c)
            send(out, here, d3s.at[g, k], d3r.at[g, k], me_n, partner)

    def pass_across(g):
        j0, jn = dgroups[g]
        js = pl.ds(j0, jn)
        for k in near_first:
            src = node_at(-k)
            for d in range(1, nx):
                here = block(js, x_at(-d) * 2 + me_c, src)
                remote(here, here, d2s.at[g, k, d], d2r.at[g, k, d], me_n, partner).wait_recv()
                send(here, here, d4s.at[g, k, d], d4r.at[g, k, d], me_n, partner)

    def wait_rest(g):
        j0, jn = dgroups[g]
        js = pl.ds(j0, jn)
        own[g].wait()
        for k in near_first:
            src = node_at(-k)
            here = block(js, partner, src)
            remote(here, here, d3s.at[g, k], d3r.at[g, k], me_n, partner).wait_recv()
            for d in range(1, nx):
                here = block(js, x_at(-d) * 2 + (1 - me_c), src)
                remote(here, here, d4s.at[g, k, d], d4r.at[g, k, d], me_n, partner).wait_recv()

    acc = (jnp.zeros((rows, ff), f32), jnp.zeros((rows, ff), f32))

    def first_matmuls(g, acc):
        j0, jn = dgroups[g]

        def step(j, acc):
            x = from_tiles(rx[j].reshape(rows, SUB, LANE), rows)
            ks = pl.ds(pl.multiple_of(j * COLS, COLS), COLS)
            return (acc[0] + jnp.dot(x, wg[ks, :], preferred_element_type=f32),
                    acc[1] + jnp.dot(x, wu[ks, :], preferred_element_type=f32))
        return lax.fori_loop(j0, j0 + jn, step, acc)

    for g in range(len(dgroups)):
        pass_on(g)
        if g > 0:
            pass_across(g - 1)
    pass_across_last = len(dgroups) - 1
    for g in range(len(dgroups)):
        if g == pass_across_last:
            pass_across(g)
        wait_rest(g)
        if g == 0:
            loads[0].wait()
            loads[1].wait()
        acc = first_matmuls(g, acc)
    hidden = (acc[0] / (1.0 + jnp.exp(-acc[0])) * acc[1]).astype(bf16)
    loads[2].wait()

    octs = per // SUB
    for g, (j0, jn) in enumerate(cgroups):
        js = pl.ds(j0, jn)
        for j in range(j0, j0 + jn):
            y = jnp.dot(hidden, wd[:, j * COLS:(j + 1) * COLS], preferred_element_type=f32)
            py[j] = y.reshape(n_local, octs, SUB, COLS).astype(bf16)
        for xx in range(nx):
            send(py.at[js, xx * 2 + (1 - me_c)], r1b.at[js, xx], r1s.at[g, xx], r1r.at[g, xx], me_n, partner)
    for g, (j0, jn) in enumerate(cgroups):
        js = pl.ds(j0, jn)
        for xx in range(nx):
            there = r1b.at[js, xx]
            remote(there, there, r1s.at[g, xx], r1r.at[g, xx], me_n, partner).wait_recv()
        for d in range(1, nx):
            xd = x_at(d)
            for j in range(j0, j0 + jn):
                s2[j, d - 1] = (py[j, xd * 2 + me_c].astype(f32) + r1b[j, xd].astype(f32)).astype(bf16)
            send(s2.at[js, d - 1], r2b.at[js, d - 1], r2s.at[g, d], r2r.at[g, d], me_n, xd * 2 + me_c)
    back = []
    for g, (j0, jn) in enumerate(cgroups):
        js = pl.ds(j0, jn)
        for d in range(1, nx):
            there = r2b.at[js, d - 1]
            remote(there, there, r2s.at[g, d], r2r.at[g, d], me_n, partner).wait_recv()
        for j in range(j0, j0 + jn):
            total = py[j, me_l].astype(f32) + r1b[j, me_x].astype(f32)
            for d in range(1, nx):
                total = total + r2b[j, d - 1].astype(f32)
            a3[j] = to_tiles(total.reshape(per, COLS), per)
        for k in far_first:
            dst = node_at(k)
            send(a3.at[js, pl.ds(dst * SLOT, SLOT)], ax.at[js, mine_rows],
                 r3s.at[g, k], r3r.at[g, k], dst, me_l)
        copy = pltpu.make_async_copy(a3.at[js, mine_rows], ax.at[js, mine_rows], bsem.at[g])
        copy.start()
        back.append(copy)
    for g, (j0, jn) in enumerate(cgroups):
        js = pl.ds(j0, jn)
        back[g].wait()
        for k in near_first[1:]:
            there = ax.at[js, pl.ds(node_at(-k) * SLOT, SLOT)]
            remote(there, there, r3s.at[g, k], r3r.at[g, k], me_n, partner).wait_recv()
        for j in range(j0, j0 + jn):
            answers = from_tiles(ax[j], per)
            out_ref[0:per, j * COLS:(j + 1) * COLS] = answers
            out_ref[padded:padded + per, j * COLS:(j + 1) * COLS] = answers
    for copy in sent:
        copy.wait_send()


def mix(place_ref, answers_ref, out_ref):
    answers = answers_ref[...]
    mixed = (jnp.dot(place_ref[0], answers, preferred_element_type=jnp.float32)
             + jnp.dot(place_ref[1], answers, preferred_element_type=jnp.float32))
    out_ref[...] = mixed.astype(out_ref.dtype)


def shards(n_node, n_local, tokens, w_gate, w_up, w_down, chosen, counts, gates):
    tok_dev, width = tokens.shape
    ff = w_gate.shape[2]
    chunks = width // COLS
    nx = n_local // 2
    per = n_node * SLOT
    octs = per // SUB
    padded = -(-per // 16) * 16
    rows = n_local * per
    dg, cg = len(split(chunks, DISPATCH_GROUPS)), len(split(chunks, COMBINE_GROUPS))
    bf16 = jnp.bfloat16
    vmem = pl.BlockSpec(memory_space=pltpu.VMEM)
    dma = pltpu.SemaphoreType.DMA
    xs = max(nx - 1, 1)
    answers, place = pl.pallas_call(
        functools.partial(kernel, (n_node, n_local, chunks, tok_dev, ff)),
        out_shape=(jax.ShapeDtypeStruct((2 * padded, width), bf16), jax.ShapeDtypeStruct((tok_dev, 2 * padded), bf16)),
        in_specs=[pl.BlockSpec(memory_space=pl.ANY)] * 7,
        out_specs=(vmem, vmem),
        scratch_shapes=[
            pltpu.SMEM(counts.shape, counts.dtype),
            pltpu.VMEM(chosen.shape, chosen.dtype),
            pltpu.VMEM(gates.shape, gates.dtype),
            pltpu.VMEM((tok_dev, width), bf16),
            pltpu.VMEM((width, ff), bf16),
            pltpu.VMEM((width, ff), bf16),
            pltpu.VMEM((ff, width), bf16),
            pltpu.VMEM((chunks, per, SUB, LANE), bf16),
            pltpu.VMEM((chunks, n_local, per, SUB, LANE), bf16),
            pltpu.VMEM((chunks, n_local, octs, SUB, COLS), bf16),
            pltpu.VMEM((chunks, nx, octs, SUB, COLS), bf16),
            pltpu.VMEM((chunks, xs, octs, SUB, COLS), bf16),
            pltpu.VMEM((chunks, xs, octs, SUB, COLS), bf16),
            pltpu.VMEM((chunks, per, SUB, LANE), bf16),
            pltpu.VMEM((chunks, per, SUB, LANE), bf16),
            pltpu.VMEM((rows * SUB, LANE), jnp.float32),
            dma((7,)), dma((dg,)), dma((cg,)),
            dma((dg, n_node)), dma((dg, n_node)),
            dma((dg, n_node, nx)), dma((dg, n_node, nx)),
            dma((dg, n_node)), dma((dg, n_node)),
            dma((dg, n_node, nx)), dma((dg, n_node, nx)),
            dma((cg, nx)), dma((cg, nx)),
            dma((cg, nx)), dma((cg, nx)),
            dma((cg, n_node)), dma((cg, n_node)),
        ],
        compiler_params=pltpu.CompilerParams(
            collective_id=0, has_side_effects=True, vmem_limit_bytes=66000000),
    )(counts, chosen, gates, tokens, w_gate, w_up, w_down)
    return jnp.dot(place, answers, preferred_element_type=jnp.float32).astype(bf16)


def solution(mesh):
    in_specs = (
        P(("node", "local"), None),
        P("node", None, "local"),
        P("node", None, "local"),
        P("node", "local", None),
        P(),
        P(),
        P(),
    )
    out_specs = P(("node", "local"), None)
    body = functools.partial(shards, mesh.shape["node"], mesh.shape["local"])
    return jax.shard_map(body, mesh=mesh, in_specs=in_specs, out_specs=out_specs, check_vma=False)
```

profile of v0, /device:TPU:0, one launch (start us, length us, event | category | flops | bytes accessed | tf_op | source)
XLA Modules:
  0.0 42.9 jit_solution(5504162826252578122)
XLA Ops:
  0.0 39.9 %shard_map.73 = (bf16[64,7168]{1,0:T(8,128)(2,1)}, bf16[128,64]{1,0:T(8,128)(2,1)}) custom-call(s32[8]{0:T(128)} %counts_hbm.1, s32[8,48]{1,0:T(8,128)} %chosen_hbm.1, f32[8,48]{1,0:T(8,128)} %gates_hbm.1, bf16[128,7168]{1,0:T(8,128)(2,1)} %tokens_hbm.1, bf16[1,7168,256]{2,1,0:T(8,128)(2,1)} %wg_hbm.1, bf16[1,7168,256]{2,1,0:T(8,128)(2,1)} %wu_hbm.1, ...), custom_call_target="tpu_custom_call" | custom-call | tf_op jit(solution)/shard_map/pallas_call | solution.py:289
  39.9 3.0 %convolution_convert_fusion = bf16[128,7168]{1,0:T(8,128)(2,1)} fusion(bf16[128,64]{1,0:T(8,128)(2,1)} %get-tuple-element.7, bf16[64,7168]{1,0:T(8,128)(2,1)} %get-tuple-element.8), kind=kOutput, calls=%fused_computation | convolution fusion | flops 118358016 | bytes 2768896 | tf_op jit(solution)/shard_map/dot_general | solution.py:323
where the time goes:
time: 43.1 us; the launch traced here: 42.9 us
  Pallas kernels  39.9 us (93%)
  matrix products  3.05 us (7%)
    pallas_call x1, Pallas kernels, shards(): pl.pallas_call(functools.partial(kernel, (n_node, n_local, chunks, tok_de...  39.9 us
    dot_general x1, matrix products, shards(): jnp.dot(place, answers, preferred_element_type=jnp.float32).astype(bf16)  3.05 us

commit v1 on v0

v1 whole, which is shorter than its diff:
```python
import functools

import jax
import jax.numpy as jnp
from jax import lax
from jax.experimental import pallas as pl
from jax.experimental.pallas import tpu as pltpu
from jax.sharding import PartitionSpec as P

SLOT = 3
SUB, LANE = 8, 128
COLS = SUB * LANE
MESH = pl.DeviceIdType.MESH
BATCHES = 3
DISPATCH_GROUPS = 2
COMBINE_GROUPS = 2


def split(count, groups):
    groups = min(groups, count)
    sizes = [count // groups + (1 if g < count % groups else 0) for g in range(groups)]
    starts = [sum(sizes[:g]) for g in range(groups)]
    return list(zip(starts, sizes))


def row_order(n_node):
    far = [(k, s) for k in range(n_node - 1, n_node // 2 - 1, -1) for s in range(SLOT)]
    near = [(k, s) for k in range(n_node // 2 - 1, -1, -1) for s in range(SLOT)]
    half, rows = SUB // 2, []
    while far or near:
        rows += far[:half] + near[:half]
        far, near = far[half:], near[half:]
    return rows


def runs_of(order, first, count):
    runs = []
    for p in range(first, first + count):
        k = order[p][0]
        if runs and runs[-1][0] == k and runs[-1][1] + runs[-1][2] == p:
            runs[-1][2] += 1
        else:
            runs.append([k, p, 1])
    return [tuple(run) for run in runs]


def plan(nb, dg, cg):
    wire = 7.4 / (nb * dg)
    steps = []
    done = {}
    for b in range(nb):
        for g in range(dg):
            i = b * dg + g
            near = 2.2 + wire * (i + 1)
            across = near + 1.8 + wire
            steps.append((near, "pass_on", b, g))
            steps.append((across, "pass_across", b, g))
            steps.append((across + 1.1, "hidden", b, g))
            done[b] = across + 1.1
        start = done[b] + 0.4
        steps.append((start, "down", b, 0))
        for g in range(cg):
            steps.append((start + 1.0 + 0.3 * g, "pair_sum", b, g))
            steps.append((start + 3.4 + 1.2 * g, "answer", b, g))
    return [step[1:] for step in sorted(steps, key=lambda step: step[0])]


def kernel(dims, counts_hbm, chosen_hbm, gates_hbm, tokens_hbm, wg_hbm, wu_hbm, wd_hbm, out_ref,
           counts_ref, chosen_ref, gates_ref, tokens_ref, wg, wu, wd, tx, rx, py, r1b, s2, r2b, a3, ax, stage,
           wsem, ssem, d1, d2, d3, c1, c2, c3):
    n_node, n_local, chunks, tok_dev, ff = dims
    nx = n_local // 2
    experts, cap = chosen_ref.shape
    per = n_node * SLOT
    octs = per // SUB
    f32, bf16 = jnp.float32, jnp.bfloat16
    me_n, me_l = lax.axis_index("node"), lax.axis_index("local")
    me_x, me_c = me_l // 2, me_l % 2
    mine, half, other = me_c * nx + me_x, me_c * nx, (1 - me_c) * nx
    partner = me_x * 2 + (1 - me_c)
    order = row_order(n_node)
    batches = split(octs, BATCHES)
    dgroups, cgroups = split(chunks, DISPATCH_GROUPS), split(chunks, COMBINE_GROUPS)

    paired = n_node & (n_node - 1) == 0

    def node_at(k):
        if paired:
            return jnp.bitwise_xor(me_n, abs(k))
        return lax.rem(me_n + k + n_node, n_node)

    def x_at(k):
        return lax.rem(me_x + k + nx, nx)

    def remote(src, dst, ssem, rsem, node, local):
        return pltpu.make_async_remote_copy(
            src_ref=src, dst_ref=dst, send_sem=ssem, recv_sem=rsem,
            device_id=(node, local), device_id_type=MESH)

    def send(*args):
        remote(*args).start()

    def arrived(ref, sem):
        remote(ref, ref, sem, sem, me_n, partner).wait_recv()

    barrier = pltpu.get_barrier_semaphore()
    for k in range(1, n_node):
        pl.semaphore_signal(barrier, inc=1, device_id=(node_at(k), me_l), device_id_type=MESH)
    pl.semaphore_signal(barrier, inc=1, device_id=(me_n, partner), device_id_type=MESH)
    for k in range(1, nx):
        pl.semaphore_signal(barrier, inc=1, device_id=(me_n, x_at(k) * 2 + me_c), device_id_type=MESH)

    loads = [pltpu.make_async_copy(src, dst, wsem.at[i]) for i, (src, dst) in enumerate((
        (wg_hbm.at[0], wg), (wu_hbm.at[0], wu), (wd_hbm.at[0], wd), (tokens_hbm, tokens_ref),
        (counts_hbm, counts_ref), (chosen_hbm, chosen_ref), (gates_hbm, gates_ref)))]
    for copy in loads[4:] + [loads[3]] + loads[:3]:
        copy.start()
    for copy in loads[4:]:
        copy.wait()

    base = (me_n * n_local + me_l) * tok_dev
    row = lax.broadcasted_iota(jnp.int32, (experts, cap), 0)
    count = jnp.zeros((experts, cap), jnp.int32)
    for e in range(experts):
        count = jnp.where(row == e, counts_ref[e], count)
    pos = chosen_ref[...] - base
    live = (lax.broadcasted_iota(jnp.int32, (experts, cap), 1) < count) & (pos >= 0) & (pos < tok_dev)
    before = (lax.broadcasted_iota(jnp.int32, (cap, cap), 0)
              < lax.broadcasted_iota(jnp.int32, (cap, cap), 1))
    rank = jnp.dot(jnp.where(live, 1.0, 0.0).astype(bf16), jnp.where(before, 1.0, 0.0).astype(bf16),
                   preferred_element_type=f32)
    pos1 = (pos + 1).astype(f32)
    lane1 = (lax.broadcasted_iota(jnp.int32, (experts, tok_dev), 1) + 1).astype(f32)
    hits = []
    for s in range(SLOT):
        where = jnp.sum(jnp.where(live & (rank == float(s)), pos1, 0.0), axis=1, keepdims=True)
        hits.append(lane1 == where)
    pick = jnp.concatenate([jnp.where(hit, 1.0, 0.0) for hit in hits], axis=0)
    col = lax.broadcasted_iota(jnp.int32, (per, per), 1)
    source = lax.broadcasted_iota(jnp.int32, (per, per), 0)
    wanted = jnp.zeros((per, per), jnp.int32)
    for p, (k, s) in enumerate(order):
        wanted = jnp.where(source == p, node_at(k) + s * experts, wanted)
    permute = jnp.where(col == wanted, 1.0, 0.0).astype(bf16)

    def ordered(x):
        return jnp.dot(permute, x, preferred_element_type=f32)

    select = ordered(pick.astype(bf16)).astype(bf16)

    def to_tiles(value, m, side):
        for q in range(SUB):
            stage[side, pl.ds(q, m, stride=SUB), :] = value[:, q * LANE:(q + 1) * LANE]
        return stage[side, pl.ds(0, m * SUB), :].astype(bf16).reshape(m, SUB, LANE)

    def from_tiles(value, m, side, times=1):
        stage[side, pl.ds(0, m * SUB), :] = value.reshape(m * SUB, LANE).astype(f32)
        parts = [stage[side, pl.ds(q, m, stride=SUB), :] for q in range(SUB)]
        return jnp.concatenate([jnp.concatenate([p] * times, axis=0).astype(bf16) for p in parts], axis=1)

    def send_rows(src, dst, b, js, sems, sent, back):
        o0, on = batches[b]
        for k, p, n in runs_of(order, o0 * SUB, on * SUB):
            if k:
                send(src.at[js, pl.ds(p, n)], dst.at[js, pl.ds(p, n)] if back else dst.at[js, mine, pl.ds(p, n)],
                     sent, sems, node_at(-k if back else k), me_l)

    def remote_rows(b):
        o0, on = batches[b]
        return sum(n for k, _, n in runs_of(order, o0 * SUB, on * SUB) if k)

    def own_rows(b):
        o0, on = batches[b]
        return [(p, n) for k, p, n in runs_of(order, o0 * SUB, on * SUB) if not k]

    loads[3].wait()
    for g, (j0, jn) in enumerate(dgroups):
        for j in range(j0, j0 + jn):
            picked = jnp.dot(select, tokens_ref[:, j * COLS:(j + 1) * COLS], preferred_element_type=f32)
            tiles = to_tiles(picked, per, j % 2)
            tx[j] = tiles
            for b in range(len(batches)):
                for p, n in own_rows(b):
                    rx[j, mine, p:p + n] = tiles[p:p + n]
        if g == 0:
            pl.semaphore_wait(barrier, n_node - 1 + 1 + nx - 1)
        send_rows(tx, rx, 0, pl.ds(j0, jn), d1.at[0, g], ssem.at[0], False)
    for b in range(1, len(batches)):
        for g, (j0, jn) in enumerate(dgroups):
            send_rows(tx, rx, b, pl.ds(j0, jn), d1.at[b, g], ssem.at[0], False)

    weight = jnp.concatenate([
        jnp.where(hits[s], jnp.sum(jnp.where(live & (rank == float(s)), gates_ref[...], 0.0), axis=1, keepdims=True), 0.0)
        for s in range(SLOT)], axis=0)
    high = weight.astype(bf16)
    low = (weight - high.astype(f32)).astype(bf16)
    place = jnp.transpose(jnp.concatenate([ordered(high), ordered(low)], axis=0)).astype(bf16)

    hidden_of = {}

    def pass_on(b, g):
        o0, on = batches[b]
        js, rows = pl.ds(*dgroups[g]), pl.ds(o0 * SUB, on * SUB)
        arrived(rx.at[js, mine, pl.ds(o0 * SUB, remote_rows(b))], d1.at[b, g])
        block = rx.at[js, mine, rows]
        for d in range(1, nx):
            send(block, block, ssem.at[1], d2.at[b, g], me_n, x_at(d) * 2 + me_c)
        send(block, block, ssem.at[2], d3.at[b, g], me_n, partner)

    def pass_across(b, g):
        o0, on = batches[b]
        js, rows = pl.ds(*dgroups[g]), pl.ds(o0 * SUB, on * SUB)
        arrived(rx.at[js, pl.ds(half, nx - 1), rows], d2.at[b, g])
        for d in range(1, nx):
            block = rx.at[js, half + x_at(-d), rows]
            send(block, block, ssem.at[2], d3.at[b, g], me_n, partner)

    def hidden(b, g):
        o0, on = batches[b]
        j0, jn = dgroups[g]
        m = n_local * on * SUB
        arrived(rx.at[pl.ds(j0, jn), pl.ds(other, nx), pl.ds(o0 * SUB, on * SUB)], d3.at[b, g])
        if b == 0 and g == 0:
            loads[0].wait()
            loads[1].wait()
        x = jnp.concatenate([
            from_tiles(rx[j, :, o0 * SUB:(o0 + on) * SUB].reshape(m, SUB, LANE), m, j % 2)
            for j in range(j0, j0 + jn)], axis=1)
        ks = pl.ds(j0 * COLS, jn * COLS)
        now = (jnp.dot(x, wg[ks, :], preferred_element_type=f32), jnp.dot(x, wu[ks, :], preferred_element_type=f32))
        old = hidden_of.get(b)
        hidden_of[b] = now if old is None else (old[0] + now[0], old[1] + now[1])

    def down(b, _):
        o0, on = batches[b]
        gate, up = hidden_of.pop(b)
        h = (gate / (1.0 + jnp.exp(-gate)) * up).astype(bf16)
        if b == 0:
            loads[2].wait()
        for g, (j0, jn) in enumerate(cgroups):
            js = pl.ds(j0, jn)
            for j in range(j0, j0 + jn):
                y = jnp.dot(h, wd[:, j * COLS:(j + 1) * COLS], preferred_element_type=f32)
                py[j, :, o0:o0 + on] = y.reshape(n_local, on, SUB, COLS).astype(bf16)
            send(py.at[js, pl.ds(other, nx), pl.ds(o0, on)], r1b.at[js, :, pl.ds(o0, on)],
                 ssem.at[3], c1.at[b, g], me_n, partner)

    def pair_sum(b, g):
        o0, on = batches[b]
        j0, jn = cgroups[g]
        js, os = pl.ds(j0, jn), pl.ds(o0, on)
        arrived(r1b.at[js, :, os], c1.at[b, g])
        for d in range(1, nx):
            xd = x_at(d)
            for j in range(j0, j0 + jn):
                s2[j, d - 1, o0:o0 + on] = (py[j, half + xd, o0:o0 + on].astype(f32)
                                            + r1b[j, xd, o0:o0 + on].astype(f32)).astype(bf16)
            send(s2.at[js, d - 1, os], r2b.at[js, d - 1, os], ssem.at[4], c2.at[b, g], me_n, xd * 2 + me_c)

    def answer(b, g):
        o0, on = batches[b]
        j0, jn = cgroups[g]
        js, os = pl.ds(j0, jn), pl.ds(o0, on)
        arrived(r2b.at[js, :, os], c2.at[b, g])
        for j in range(j0, j0 + jn):
            total = py[j, mine, o0:o0 + on].astype(f32) + r1b[j, me_x, o0:o0 + on].astype(f32)
            for d in range(1, nx):
                total = total + r2b[j, d - 1, o0:o0 + on].astype(f32)
            tiles = to_tiles(total.reshape(on * SUB, COLS), on * SUB, j % 2)
            a3[j, o0 * SUB:(o0 + on) * SUB] = tiles
            for p, n in own_rows(b):
                ax[j, p:p + n] = tiles[p - o0 * SUB:p - o0 * SUB + n]
        send_rows(a3, ax, b, js, c3.at[b, g], ssem.at[5], True)

    run = {"pass_on": pass_on, "pass_across": pass_across, "hidden": hidden, "down": down,
           "pair_sum": pair_sum, "answer": answer}
    for name, b, g in plan(len(batches), len(dgroups), len(cgroups)):
        with jax.named_scope(f"{name}_{b}{g}"):
            run[name](b, g)
    for g, (j0, jn) in enumerate(cgroups):
        with jax.named_scope(f"back_{g}"):
            for b, (o0, on) in enumerate(batches):
                arrived(ax.at[pl.ds(j0, jn), pl.ds(o0 * SUB, remote_rows(b))], c3.at[b, g])
        for j in range(j0, j0 + jn):
            answers = from_tiles(ax[j], per, j % 2, 2)
            out_ref[:, j * COLS:(j + 1) * COLS] = jnp.dot(place, answers, preferred_element_type=f32).astype(bf16)
    for i, ref in enumerate((tx.at[:, pl.ds(0, per - SLOT)], rx.at[:, pl.ds(0, nx - 1)], rx.at[:, pl.ds(0, nx)],
                             py.at[:, pl.ds(0, nx)], s2, a3.at[:, pl.ds(0, per - SLOT)])):
        remote(ref, ref, ssem.at[i], ssem.at[i], me_n, partner).wait_send()


def shards(n_node, n_local, tokens, w_gate, w_up, w_down, chosen, counts, gates):
    tok_dev, width = tokens.shape
    ff = w_gate.shape[2]
    chunks = width // COLS
    nx = n_local // 2
    per = n_node * SLOT
    octs = per // SUB
    nb, dg, cg = len(split(octs, BATCHES)), len(split(chunks, DISPATCH_GROUPS)), len(split(chunks, COMBINE_GROUPS))
    deep = max(per, n_local * SUB * split(octs, BATCHES)[0][1])
    bf16 = jnp.bfloat16
    vmem = pl.BlockSpec(memory_space=pltpu.VMEM)
    dma = pltpu.SemaphoreType.DMA
    buffers = [
        ((tok_dev, width), bf16),
        ((width, ff), bf16),
        ((width, ff), bf16),
        ((ff, width), bf16),
        ((chunks, per, SUB, LANE), bf16),
        ((chunks, n_local, per, SUB, LANE), bf16),
        ((chunks, n_local, octs, SUB, COLS), bf16),
        ((chunks, nx, octs, SUB, COLS), bf16),
        ((chunks, nx - 1, octs, SUB, COLS), bf16),
        ((chunks, nx - 1, octs, SUB, COLS), bf16),
        ((chunks, per, SUB, LANE), bf16),
        ((chunks, per, SUB, LANE), bf16),
        ((2, deep * SUB, LANE), jnp.float32),
    ]
    size = sum(functools.reduce(lambda a, b: a * b, shape) * jnp.dtype(kind).itemsize for shape, kind in buffers)
    args = (counts, chosen, gates, tokens, w_gate, w_up, w_down)
    return pl.pallas_call(
        functools.partial(kernel, (n_node, n_local, chunks, tok_dev, ff)),
        out_shape=jax.ShapeDtypeStruct((tok_dev, width), bf16),
        in_specs=[pl.BlockSpec(memory_space=pl.ANY)] * 7,
        out_specs=vmem,
        scratch_shapes=[
            pltpu.SMEM(counts.shape, counts.dtype),
            pltpu.VMEM(chosen.shape, chosen.dtype),
            pltpu.VMEM(gates.shape, gates.dtype),
            *(pltpu.VMEM(shape, kind) for shape, kind in buffers),
            dma((7,)), dma((6,)),
            dma((nb, dg)), dma((nb, dg)), dma((nb, dg)),
            dma((nb, cg)), dma((nb, cg)), dma((nb, cg)),
        ],
        compiler_params=pltpu.CompilerParams(
            collective_id=0, has_side_effects=True, vmem_limit_bytes=min(size + 14000000, 66000000)),
    )(*(pltpu.with_memory_space_constraint(arg, pltpu.HBM) for arg in args))


def solution(mesh):
    in_specs = (
        P(("node", "local"), None),
        P("node", None, "local"),
        P("node", None, "local"),
        P("node", "local", None),
        P(),
        P(),
        P(),
    )
    out_specs = P(("node", "local"), None)
    body = functools.partial(shards, mesh.shape["node"], mesh.shape["local"])
    return jax.shard_map(body, mesh=mesh, in_specs=in_specs, out_specs=out_specs, check_vma=False)
```

time: 43.1 us -> 37.6 us (0.87)
  Pallas kernels: 39.9 us -> 36.2 us
  matrix products: 3.05 us -> 0 us
  local copies, waits for them, and re-layouts: 0 us -> 1.23 us
    pallas_call x1, Pallas kernels: 39.9 us -> 36.2 us  [shards(): pl.pallas_call(functools.partial(kernel, (n_node, n_local, chunks, tok_de...]
    dot_general x1 -> x0, matrix products: 3.05 us -> none  [shards(): jnp.dot(place, answers, preferred_element_type=jnp.float32).astype(bf16)]
    unnamed x0 -> x1, local copies, waits for them, and re-layouts: none -> 1.23 us
where the time goes in v1:
time: 37.6 us; the launch traced here: 37.4 us
  Pallas kernels  36.2 us (96%)
  local copies, waits for them, and re-layouts  1.23 us (3%)
    pallas_call x1, Pallas kernels, shards(): pl.pallas_call(functools.partial(kernel, (n_node, n_local, chunks, tok_de...  36.2 us
    unnamed x1, local copies, waits for them, and re-layouts  1.23 us

profile of v1, /device:TPU:0, one launch (start us, length us, event | category | flops | bytes accessed | tf_op | source)
XLA Modules:
  0.0 37.4 jit_solution(12710225785218492833)
XLA Ops:
  0.0 36.2 %shard_map.73 = bf16[128,7168]{1,0:T(8,128)(2,1)S(1)} custom-call(s32[8]{0:T(128)} %counts_hbm.1, s32[8,48]{1,0:T(8,128)} %chosen_hbm.1, f32[8,48]{1,0:T(8,128)} %gates_hbm.1, bf16[128,7168]{1,0:T(8,128)(2,1)} %tokens_hbm.1, bf16[1,7168,256]{2,1,0:T(8,128)(2,1)} %wg_hbm.1, bf16[1,7168,256]{2,1,0:T(8,128)(2,1)} %wu_hbm.1, bf16[1,256,7168]{2,1,0:T(8,128)(2,1)} %wd_hbm.1), custom_call_target="tpu_custom_call" | custom-call | tf_op jit(solution)/shard_map/pallas_call | solution.py:321
  36.2 1.2 %copy.9 = bf16[128,7168]{1,0:T(8,128)(2,1)} copy(bf16[128,7168]{1,0:T(8,128)(2,1)S(1)} %shard_map.73) | data formatting | bytes 3670016

commit v2 on v1

--- a/solution.py
+++ b/solution.py
@@ -12,8 +12,9 @@
 COLS = SUB * LANE
 MESH = pl.DeviceIdType.MESH
 BATCHES = 3
-DISPATCH_GROUPS = 2
-COMBINE_GROUPS = 2
+ACROSS, HOP, NEAR, NEAR_STEP, FAR, FAR_STEP = 2.6, 1.0, 2.2, 0.7, 2.2, 0.75
+DISPATCH_GROUPS = 3
+COMBINE_GROUPS = 3
 
 
 def split(count, groups):
@@ -23,13 +24,19 @@
     return list(zip(starts, sizes))
 
 
+def batches_of(n_node):
+    sizes = sorted(count for _, count in split(n_node * SLOT // SUB, BATCHES))
+    return [(sum(sizes[:b]), size) for b, size in enumerate(sizes)]
+
+
 def row_order(n_node):
     far = [(k, s) for k in range(n_node - 1, n_node // 2 - 1, -1) for s in range(SLOT)]
     near = [(k, s) for k in range(n_node // 2 - 1, -1, -1) for s in range(SLOT)]
-    half, rows = SUB // 2, []
-    while far or near:
-        rows += far[:half] + near[:half]
-        far, near = far[half:], near[half:]
+    rows = []
+    for _, octs in batches_of(n_node):
+        half = max(octs * SUB // 2, octs * SUB - len(near))
+        rows += far[:half] + near[:octs * SUB - half]
+        far, near = far[half:], near[octs * SUB - half:]
     return rows
 
 
@@ -44,29 +51,52 @@
     return [tuple(run) for run in runs]
 
 
-def plan(nb, dg, cg):
-    wire = 7.4 / (nb * dg)
-    steps = []
-    done = {}
+def plan(sizes, dg, cg):
+    nb, total = len(sizes), sum(sizes)
+    wire = [7.0 * size / total / dg for size in sizes]
+    work = {"pass_near": 0.02, "pass_far": 0.02, "pass_across": 0.02, "pair_sum": 0.03, "answer": 0.05,
+            "hidden": 1.65 / dg, "down": 1.0 / cg}
+    rank = {name: i for i, name in enumerate(("pass_far", "pass_near", "pass_across", "pair_sum", "answer", "hidden", "down"))}
+    ready = {}
+    passed = 0.0
     for b in range(nb):
         for g in range(dg):
-            i = b * dg + g
-            near = 2.2 + wire * (i + 1)
-            across = near + 1.8 + wire
-            steps.append((near, "pass_on", b, g))
-            steps.append((across, "pass_across", b, g))
-            steps.append((across + 1.1, "hidden", b, g))
-            done[b] = across + 1.1
-        start = done[b] + 0.4
-        steps.append((start, "down", b, 0))
-        for g in range(cg):
-            steps.append((start + 1.0 + 0.3 * g, "pair_sum", b, g))
-            steps.append((start + 3.4 + 1.2 * g, "answer", b, g))
-    return [step[1:] for step in sorted(steps, key=lambda step: step[0])]
+            ready["pass_near", b, g] = NEAR + NEAR_STEP * passed
+            passed += 9 * sizes[b] / total / dg
+            ready["pass_far", b, g] = FAR + FAR_STEP * passed
+    steps, clock, link = [], 0.0, 0.0
+
+    def urgency(step):
+        name, b, g = step
+        return (b + 4 if name in ("hidden", "down") else 0, rank[name], b, g)
+
+    while ready:
+        clock = max(clock, min(ready.values()))
+        name, b, g = step = min((s for s in ready if ready[s] <= clock), key=urgency)
+        del ready[step]
+        steps.append(step)
+        clock += work[name]
+        if name in ("pass_near", "pass_far"):
+            link = max(link, clock) + wire[b] / 2
+            if not any(("pass_far" if name == "pass_near" else "pass_near", b, g) == s for s in ready):
+                ready["pass_across", b, g] = link + ACROSS
+        elif name == "pass_across":
+            ready["hidden", b, g] = clock + HOP
+        elif name == "hidden":
+            if g == dg - 1:
+                ready["down", b, 0] = clock
+        elif name == "down":
+            ready["pair_sum", b, g] = clock + HOP
+            if g < cg - 1:
+                ready["down", b, g + 1] = clock
+        elif name == "pair_sum":
+            link = max(link, clock) + wire[b] * dg / cg
+            ready["answer", b, g] = link + ACROSS
+    return steps
 
 
 def kernel(dims, counts_hbm, chosen_hbm, gates_hbm, tokens_hbm, wg_hbm, wu_hbm, wd_hbm, out_ref,
-           counts_ref, chosen_ref, gates_ref, tokens_ref, wg, wu, wd, tx, rx, py, r1b, s2, r2b, a3, ax, stage,
+           counts_ref, chosen_ref, gates_ref, tokens_ref, wgu, wd, tx, rx, py, r1b, s2, r2b, a3, ax, stage,
            wsem, ssem, d1, d2, d3, c1, c2, c3):
     n_node, n_local, chunks, tok_dev, ff = dims
     nx = n_local // 2
@@ -79,7 +109,7 @@
     mine, half, other = me_c * nx + me_x, me_c * nx, (1 - me_c) * nx
     partner = me_x * 2 + (1 - me_c)
     order = row_order(n_node)
-    batches = split(octs, BATCHES)
+    batches = batches_of(n_node)
     dgroups, cgroups = split(chunks, DISPATCH_GROUPS), split(chunks, COMBINE_GROUPS)
 
     paired = n_node & (n_node - 1) == 0
@@ -111,11 +141,12 @@
         pl.semaphore_signal(barrier, inc=1, device_id=(me_n, x_at(k) * 2 + me_c), device_id_type=MESH)
 
     loads = [pltpu.make_async_copy(src, dst, wsem.at[i]) for i, (src, dst) in enumerate((
-        (wg_hbm.at[0], wg), (wu_hbm.at[0], wu), (wd_hbm.at[0], wd), (tokens_hbm, tokens_ref),
-        (counts_hbm, counts_ref), (chosen_hbm, chosen_ref), (gates_hbm, gates_ref)))]
-    for copy in loads[4:] + [loads[3]] + loads[:3]:
+        (wg_hbm.at[0], wgu.at[:, 0:ff]), (wu_hbm.at[0], wgu.at[:, ff:2 * ff]), (wd_hbm.at[0], wd),
+        (counts_hbm, counts_ref), (chosen_hbm, chosen_ref), (gates_hbm, gates_ref),
+        *((tokens_hbm.at[:, j0 * COLS:(j0 + jn) * COLS], tokens_ref.at[:, j0 * COLS:(j0 + jn) * COLS]) for j0, jn in dgroups)))]
+    for copy in loads[3:]:
         copy.start()
-    for copy in loads[4:]:
+    for copy in loads[3:5]:
         copy.wait()
 
     base = (me_n * n_local + me_l) * tok_dev
@@ -158,23 +189,41 @@
         parts = [stage[side, pl.ds(q, m, stride=SUB), :] for q in range(SUB)]
         return jnp.concatenate([jnp.concatenate([p] * times, axis=0).astype(bf16) for p in parts], axis=1)
 
-    def send_rows(src, dst, b, js, sems, sent, back):
-        o0, on = batches[b]
-        for k, p, n in runs_of(order, o0 * SUB, on * SUB):
+    def runs(b):
+        o0, on = batches[b]
+        return runs_of(order, o0 * SUB, on * SUB)
+
+    def is_far(k):
+        return 2 * k >= n_node
+
+    def part(b, far):
+        o0, on = batches[b]
+        count = sum(n for k, _, n in runs(b) if is_far(k))
+        if far:
+            return o0 * SUB, count, sum(n for k, _, n in runs(b) if k and is_far(k))
+        return o0 * SUB + count, on * SUB - count, sum(n for k, _, n in runs(b) if k and not is_far(k))
+
+    def remote_rows(b):
+        return sum(n for k, _, n in runs(b) if k)
+
+    def own_rows(b):
+        return [(p, n) for k, p, n in runs(b) if not k]
+
+    def send_out(b, g):
+        js = pl.ds(*dgroups[g])
+        for k, p, n in runs(b):
             if k:
-                send(src.at[js, pl.ds(p, n)], dst.at[js, pl.ds(p, n)] if back else dst.at[js, mine, pl.ds(p, n)],
-                     sent, sems, node_at(-k if back else k), me_l)
-
-    def remote_rows(b):
-        o0, on = batches[b]
-        return sum(n for k, _, n in runs_of(order, o0 * SUB, on * SUB) if k)
-
-    def own_rows(b):
-        o0, on = batches[b]
-        return [(p, n) for k, p, n in runs_of(order, o0 * SUB, on * SUB) if not k]
-
-    loads[3].wait()
+                send(tx.at[js, pl.ds(p, n)], rx.at[js, mine, pl.ds(p, n)], ssem.at[0],
+                     d1.at[b, g, 1 if is_far(k) else 0], node_at(k), me_l)
+
+    def send_back(b, g):
+        js = pl.ds(*cgroups[g])
+        for k, p, n in runs(b):
+            if k:
+                send(a3.at[js, pl.ds(p, n)], ax.at[js, pl.ds(p, n)], ssem.at[5], c3.at[b, g], node_at(-k), me_l)
+
     for g, (j0, jn) in enumerate(dgroups):
+        loads[6 + g].wait()
         for j in range(j0, j0 + jn):
             picked = jnp.dot(select, tokens_ref[:, j * COLS:(j + 1) * COLS], preferred_element_type=f32)
             tiles = to_tiles(picked, per, j % 2)
@@ -184,11 +233,14 @@
                     rx[j, mine, p:p + n] = tiles[p:p + n]
         if g == 0:
             pl.semaphore_wait(barrier, n_node - 1 + 1 + nx - 1)
-        send_rows(tx, rx, 0, pl.ds(j0, jn), d1.at[0, g], ssem.at[0], False)
+        send_out(0, g)
+    for copy in loads[:3]:
+        copy.start()
     for b in range(1, len(batches)):
-        for g, (j0, jn) in enumerate(dgroups):
-            send_rows(tx, rx, b, pl.ds(j0, jn), d1.at[b, g], ssem.at[0], False)
-
+        for g in range(len(dgroups)):
+            send_out(b, g)
+
+    loads[5].wait()
     weight = jnp.concatenate([
         jnp.where(hits[s], jnp.sum(jnp.where(live & (rank == float(s)), gates_ref[...], 0.0), axis=1, keepdims=True), 0.0)
         for s in range(SLOT)], axis=0)
@@ -196,16 +248,18 @@
     low = (weight - high.astype(f32)).astype(bf16)
     place = jnp.transpose(jnp.concatenate([ordered(high), ordered(low)], axis=0)).astype(bf16)
 
-    hidden_of = {}
-
-    def pass_on(b, g):
-        o0, on = batches[b]
-        js, rows = pl.ds(*dgroups[g]), pl.ds(o0 * SUB, on * SUB)
-        arrived(rx.at[js, mine, pl.ds(o0 * SUB, remote_rows(b))], d1.at[b, g])
-        block = rx.at[js, mine, rows]
-        for d in range(1, nx):
-            send(block, block, ssem.at[1], d2.at[b, g], me_n, x_at(d) * 2 + me_c)
-        send(block, block, ssem.at[2], d3.at[b, g], me_n, partner)
+    sums, inner = {}, {}
+
+    def pass_part(b, g, far):
+        js = pl.ds(*dgroups[g])
+        first, count, remotes = part(b, far)
+        if remotes:
+            arrived(rx.at[js, mine, pl.ds(first, remotes)], d1.at[b, g, 1 if far else 0])
+        if count:
+            block = rx.at[js, mine, pl.ds(first, count)]
+            for d in range(1, nx):
+                send(block, block, ssem.at[1], d2.at[b, g], me_n, x_at(d) * 2 + me_c)
+            send(block, block, ssem.at[2], d3.at[b, g], me_n, partner)
 
     def pass_across(b, g):
         o0, on = batches[b]
@@ -227,23 +281,23 @@
             from_tiles(rx[j, :, o0 * SUB:(o0 + on) * SUB].reshape(m, SUB, LANE), m, j % 2)
             for j in range(j0, j0 + jn)], axis=1)
         ks = pl.ds(j0 * COLS, jn * COLS)
-        now = (jnp.dot(x, wg[ks, :], preferred_element_type=f32), jnp.dot(x, wu[ks, :], preferred_element_type=f32))
-        old = hidden_of.get(b)
-        hidden_of[b] = now if old is None else (old[0] + now[0], old[1] + now[1])
-
-    def down(b, _):
-        o0, on = batches[b]
-        gate, up = hidden_of.pop(b)
-        h = (gate / (1.0 + jnp.exp(-gate)) * up).astype(bf16)
-        if b == 0:
+        now = jnp.dot(x, wgu[ks, :], preferred_element_type=f32)
+        sums[b] = sums[b] + now if b in sums else now
+        if g == len(dgroups) - 1:
+            gate, up = sums[b][:, 0:ff], sums[b][:, ff:2 * ff]
+            inner[b] = (gate / (1.0 + jnp.exp(-gate)) * up).astype(bf16)
+
+    def down(b, g):
+        o0, on = batches[b]
+        j0, jn = cgroups[g]
+        if b == 0 and g == 0:
             loads[2].wait()
-        for g, (j0, jn) in enumerate(cgroups):
-            js = pl.ds(j0, jn)
-            for j in range(j0, j0 + jn):
-                y = jnp.dot(h, wd[:, j * COLS:(j + 1) * COLS], preferred_element_type=f32)
-                py[j, :, o0:o0 + on] = y.reshape(n_local, on, SUB, COLS).astype(bf16)
-            send(py.at[js, pl.ds(other, nx), pl.ds(o0, on)], r1b.at[js, :, pl.ds(o0, on)],
-                 ssem.at[3], c1.at[b, g], me_n, partner)
+        for j in range(j0, j0 + jn):
+            y = jnp.dot(inner[b], wd[:, j * COLS:(j + 1) * COLS], preferred_element_type=f32)
+            py[j, :, o0:o0 + on] = y.reshape(n_local, on, SUB, COLS).astype(bf16)
+        js = pl.ds(j0, jn)
+        send(py.at[js, pl.ds(other, nx), pl.ds(o0, on)], r1b.at[js, :, pl.ds(o0, on)],
+             ssem.at[3], c1.at[b, g], me_n, partner)
 
     def pair_sum(b, g):
         o0, on = batches[b]
@@ -270,11 +324,11 @@
             a3[j, o0 * SUB:(o0 + on) * SUB] = tiles
             for p, n in own_rows(b):
                 ax[j, p:p + n] = tiles[p - o0 * SUB:p - o0 * SUB + n]
-        send_rows(a3, ax, b, js, c3.at[b, g], ssem.at[5], True)
-
-    run = {"pass_on": pass_on, "pass_across": pass_across, "hidden": hidden, "down": down,
+        send_back(b, g)
+
+    run = {"pass_near": functools.partial(pass_part, far=False), "pass_far": functools.partial(pass_part, far=True), "pass_across": pass_across, "hidden": hidden, "down": down,
            "pair_sum": pair_sum, "answer": answer}
-    for name, b, g in plan(len(batches), len(dgroups), len(cgroups)):
+    for name, b, g in plan([on for _, on in batches], len(dgroups), len(cgroups)):
         with jax.named_scope(f"{name}_{b}{g}"):
             run[name](b, g)
     for g, (j0, jn) in enumerate(cgroups):
@@ -297,14 +351,13 @@
     per = n_node * SLOT
     octs = per // SUB
     nb, dg, cg = len(split(octs, BATCHES)), len(split(chunks, DISPATCH_GROUPS)), len(split(chunks, COMBINE_GROUPS))
-    deep = max(per, n_local * SUB * split(octs, BATCHES)[0][1])
+    deep = max(per, n_local * SUB * batches_of(n_node)[-1][1])
     bf16 = jnp.bfloat16
     vmem = pl.BlockSpec(memory_space=pltpu.VMEM)
     dma = pltpu.SemaphoreType.DMA
     buffers = [
         ((tok_dev, width), bf16),
-        ((width, ff), bf16),
-        ((width, ff), bf16),
+        ((width, 2 * ff), bf16),
         ((ff, width), bf16),
         ((chunks, per, SUB, LANE), bf16),
         ((chunks, n_local, per, SUB, LANE), bf16),
@@ -328,8 +381,8 @@
             pltpu.VMEM(chosen.shape, chosen.dtype),
             pltpu.VMEM(gates.shape, gates.dtype),
             *(pltpu.VMEM(shape, kind) for shape, kind in buffers),
-            dma((7,)), dma((6,)),
-            dma((nb, dg)), dma((nb, dg)), dma((nb, dg)),
+            dma((6 + dg,)), dma((6,)),
+            dma((nb, dg, 2)), dma((nb, dg)), dma((nb, dg)),
             dma((nb, cg)), dma((nb, cg)), dma((nb, cg)),
         ],
         compiler_params=pltpu.CompilerParams(

time: 37.6 us -> 34.4 us (0.915)
  Pallas kernels: 36.2 us -> 33 us
    pallas_call x1, Pallas kernels: 36.2 us -> 33 us  [shards(): pl.pallas_call(functools.partial(kernel, (n_node, n_local, chunks, tok_de...]
where the time goes in v2:
time: 34.4 us; the launch traced here: 34.2 us
  Pallas kernels  33 us (96%)
  local copies, waits for them, and re-layouts  1.23 us (4%)
    pallas_call x1, Pallas kernels, shards(): pl.pallas_call(functools.partial(kernel, (n_node, n_local, chunks, tok_de...  33 us
    unnamed x1, local copies, waits for them, and re-layouts  1.23 us

profile of v2, /device:TPU:0, one launch (start us, length us, event | category | flops | bytes accessed | tf_op | source)
XLA Modules:
  0.0 34.2 jit_solution(8015127664514605471)
XLA Ops:
  0.0 33.0 %shard_map.73 = bf16[128,7168]{1,0:T(8,128)(2,1)S(1)} custom-call(s32[8]{0:T(128)} %counts_hbm.1, s32[8,48]{1,0:T(8,128)} %chosen_hbm.1, f32[8,48]{1,0:T(8,128)} %gates_hbm.1, bf16[128,7168]{1,0:T(8,128)(2,1)} %tokens_hbm.1, bf16[1,7168,256]{2,1,0:T(8,128)(2,1)} %wg_hbm.1, bf16[1,7168,256]{2,1,0:T(8,128)(2,1)} %wu_hbm.1, bf16[1,256,7168]{2,1,0:T(8,128)(2,1)} %wd_hbm.1), custom_call_target="tpu_custom_call" | custom-call | tf_op jit(solution)/shard_map/pallas_call | solution.py:374
  33.0 1.2 %copy.9 = bf16[128,7168]{1,0:T(8,128)(2,1)} copy(bf16[128,7168]{1,0:T(8,128)(2,1)S(1)} %shard_map.73) | data formatting | bytes 3670016

commit v3 on v2

--- a/solution.py
+++ b/solution.py
@@ -12,9 +12,9 @@
 COLS = SUB * LANE
 MESH = pl.DeviceIdType.MESH
 BATCHES = 3
-ACROSS, HOP, NEAR, NEAR_STEP, FAR, FAR_STEP = 2.6, 1.0, 2.2, 0.7, 2.2, 0.75
-DISPATCH_GROUPS = 3
-COMBINE_GROUPS = 3
+ACROSS, HOP, NEAR, NEAR_STEP, FAR, FAR_STEP = 2.6, 1.0, 2.6, 0.9, 2.2, 0.9
+EARLY = 2
+GROUPS = 3
 
 
 def split(count, groups):
@@ -51,18 +51,18 @@
     return [tuple(run) for run in runs]
 
 
-def plan(sizes, dg, cg):
+def plan(sizes, ng):
     nb, total = len(sizes), sum(sizes)
-    wire = [7.0 * size / total / dg for size in sizes]
+    wire = [7.0 * size / total / ng for size in sizes]
     work = {"pass_near": 0.02, "pass_far": 0.02, "pass_across": 0.02, "pair_sum": 0.03, "answer": 0.05,
-            "hidden": 1.65 / dg, "down": 1.0 / cg}
+            "hidden": 1.65 / ng, "down": 1.0 / ng}
     rank = {name: i for i, name in enumerate(("pass_far", "pass_near", "pass_across", "pair_sum", "answer", "hidden", "down"))}
     ready = {}
     passed = 0.0
     for b in range(nb):
-        for g in range(dg):
+        for g in range(ng):
             ready["pass_near", b, g] = NEAR + NEAR_STEP * passed
-            passed += 9 * sizes[b] / total / dg
+            passed += 9 * sizes[b] / total / ng
             ready["pass_far", b, g] = FAR + FAR_STEP * passed
     steps, clock, link = [], 0.0, 0.0
 
@@ -75,7 +75,7 @@
         name, b, g = step = min((s for s in ready if ready[s] <= clock), key=urgency)
         del ready[step]
         steps.append(step)
-        clock += work[name]
+        clock += work[name] * ((0.55, 1.5, 0.95)[min(g, 2)] if name == "hidden" and ng == 3 else 1.0)
         if name in ("pass_near", "pass_far"):
             link = max(link, clock) + wire[b] / 2
             if not any(("pass_far" if name == "pass_near" else "pass_near", b, g) == s for s in ready):
@@ -83,21 +83,21 @@
         elif name == "pass_across":
             ready["hidden", b, g] = clock + HOP
         elif name == "hidden":
-            if g == dg - 1:
+            if g == ng - 1:
                 ready["down", b, 0] = clock
         elif name == "down":
             ready["pair_sum", b, g] = clock + HOP
-            if g < cg - 1:
+            if g < ng - 1:
                 ready["down", b, g + 1] = clock
         elif name == "pair_sum":
-            link = max(link, clock) + wire[b] * dg / cg
+            link = max(link, clock) + wire[b]
             ready["answer", b, g] = link + ACROSS
     return steps
 
 
 def kernel(dims, counts_hbm, chosen_hbm, gates_hbm, tokens_hbm, wg_hbm, wu_hbm, wd_hbm, out_ref,
            counts_ref, chosen_ref, gates_ref, tokens_ref, wgu, wd, tx, rx, py, r1b, s2, r2b, a3, ax, stage,
-           wsem, ssem, d1, d2, d3, c1, c2, c3):
+           wsem, psem, ssem, d1, d2, d3, c3):
     n_node, n_local, chunks, tok_dev, ff = dims
     nx = n_local // 2
     experts, cap = chosen_ref.shape
@@ -110,7 +110,7 @@
     partner = me_x * 2 + (1 - me_c)
     order = row_order(n_node)
     batches = batches_of(n_node)
-    dgroups, cgroups = split(chunks, DISPATCH_GROUPS), split(chunks, COMBINE_GROUPS)
+    groups = split(chunks, GROUPS)
 
     paired = n_node & (n_node - 1) == 0
 
@@ -141,12 +141,13 @@
         pl.semaphore_signal(barrier, inc=1, device_id=(me_n, x_at(k) * 2 + me_c), device_id_type=MESH)
 
     loads = [pltpu.make_async_copy(src, dst, wsem.at[i]) for i, (src, dst) in enumerate((
-        (wg_hbm.at[0], wgu.at[:, 0:ff]), (wu_hbm.at[0], wgu.at[:, ff:2 * ff]), (wd_hbm.at[0], wd),
-        (counts_hbm, counts_ref), (chosen_hbm, chosen_ref), (gates_hbm, gates_ref),
-        *((tokens_hbm.at[:, j0 * COLS:(j0 + jn) * COLS], tokens_ref.at[:, j0 * COLS:(j0 + jn) * COLS]) for j0, jn in dgroups)))]
-    for copy in loads[3:]:
+        (wd_hbm.at[0], wd), (counts_hbm, counts_ref), (chosen_hbm, chosen_ref), (gates_hbm, gates_ref),
+        *((tokens_hbm.at[:, j0 * COLS:(j0 + jn) * COLS], tokens_ref.at[:, j0 * COLS:(j0 + jn) * COLS]) for j0, jn in groups)))]
+    panels = [pltpu.make_async_copy(src.at[0, :, i * LANE:(i + 1) * LANE], wgu.at[which * (ff // LANE) + i], psem.at[0])
+              for which, src in enumerate((wg_hbm, wu_hbm)) for i in range(ff // LANE)]
+    for copy in loads[1:]:
         copy.start()
-    for copy in loads[3:5]:
+    for copy in loads[1:3]:
         copy.wait()
 
     base = (me_n * n_local + me_l) * tok_dev
@@ -203,27 +204,24 @@
             return o0 * SUB, count, sum(n for k, _, n in runs(b) if k and is_far(k))
         return o0 * SUB + count, on * SUB - count, sum(n for k, _, n in runs(b) if k and not is_far(k))
 
-    def remote_rows(b):
-        return sum(n for k, _, n in runs(b) if k)
-
     def own_rows(b):
         return [(p, n) for k, p, n in runs(b) if not k]
 
     def send_out(b, g):
-        js = pl.ds(*dgroups[g])
+        js = pl.ds(*groups[g])
         for k, p, n in runs(b):
             if k:
                 send(tx.at[js, pl.ds(p, n)], rx.at[js, mine, pl.ds(p, n)], ssem.at[0],
                      d1.at[b, g, 1 if is_far(k) else 0], node_at(k), me_l)
 
     def send_back(b, g):
-        js = pl.ds(*cgroups[g])
+        js = pl.ds(*groups[g])
         for k, p, n in runs(b):
             if k:
-                send(a3.at[js, pl.ds(p, n)], ax.at[js, pl.ds(p, n)], ssem.at[5], c3.at[b, g], node_at(-k), me_l)
-
-    for g, (j0, jn) in enumerate(dgroups):
-        loads[6 + g].wait()
+                send(a3.at[js, pl.ds(p, n)], ax.at[js, pl.ds(p, n)], ssem.at[5], c3.at[g], node_at(-k), me_l)
+
+    for g, (j0, jn) in enumerate(groups):
+        loads[4 + g].wait()
         for j in range(j0, j0 + jn):
             picked = jnp.dot(select, tokens_ref[:, j * COLS:(j + 1) * COLS], preferred_element_type=f32)
             tiles = to_tiles(picked, per, j % 2)
@@ -234,13 +232,13 @@
         if g == 0:
             pl.semaphore_wait(barrier, n_node - 1 + 1 + nx - 1)
         send_out(0, g)
-    for copy in loads[:3]:
+    for copy in [*panels, loads[0]]:
         copy.start()
-    for b in range(1, len(batches)):
-        for g in range(len(dgroups)):
+    for b in range(1, min(EARLY, len(batches))):
+        for g in range(len(groups)):
             send_out(b, g)
 
-    loads[5].wait()
+    loads[3].wait()
     weight = jnp.concatenate([
         jnp.where(hits[s], jnp.sum(jnp.where(live & (rank == float(s)), gates_ref[...], 0.0), axis=1, keepdims=True), 0.0)
         for s in range(SLOT)], axis=0)
@@ -251,7 +249,7 @@
     sums, inner = {}, {}
 
     def pass_part(b, g, far):
-        js = pl.ds(*dgroups[g])
+        js = pl.ds(*groups[g])
         first, count, remotes = part(b, far)
         if remotes:
             arrived(rx.at[js, mine, pl.ds(first, remotes)], d1.at[b, g, 1 if far else 0])
@@ -263,7 +261,7 @@
 
     def pass_across(b, g):
         o0, on = batches[b]
-        js, rows = pl.ds(*dgroups[g]), pl.ds(o0 * SUB, on * SUB)
+        js, rows = pl.ds(*groups[g]), pl.ds(o0 * SUB, on * SUB)
         arrived(rx.at[js, pl.ds(half, nx - 1), rows], d2.at[b, g])
         for d in range(1, nx):
             block = rx.at[js, half + x_at(-d), rows]
@@ -271,51 +269,51 @@
 
     def hidden(b, g):
         o0, on = batches[b]
-        j0, jn = dgroups[g]
+        j0, jn = groups[g]
         m = n_local * on * SUB
         arrived(rx.at[pl.ds(j0, jn), pl.ds(other, nx), pl.ds(o0 * SUB, on * SUB)], d3.at[b, g])
         if b == 0 and g == 0:
-            loads[0].wait()
-            loads[1].wait()
+            pltpu.make_async_copy(wgu, wgu, psem.at[0]).wait()
         x = jnp.concatenate([
             from_tiles(rx[j, :, o0 * SUB:(o0 + on) * SUB].reshape(m, SUB, LANE), m, j % 2)
             for j in range(j0, j0 + jn)], axis=1)
         ks = pl.ds(j0 * COLS, jn * COLS)
-        now = jnp.dot(x, wgu[ks, :], preferred_element_type=f32)
+        both = jnp.concatenate([wgu[i, ks, :] for i in range(2 * ff // LANE)], axis=1)
+        now = jnp.dot(x, both, preferred_element_type=f32)
         sums[b] = sums[b] + now if b in sums else now
-        if g == len(dgroups) - 1:
+        if g == len(groups) - 1:
             gate, up = sums[b][:, 0:ff], sums[b][:, ff:2 * ff]
             inner[b] = (gate / (1.0 + jnp.exp(-gate)) * up).astype(bf16)
 
     def down(b, g):
         o0, on = batches[b]
-        j0, jn = cgroups[g]
+        j0, jn = groups[g]
         if b == 0 and g == 0:
-            loads[2].wait()
+            loads[0].wait()
         for j in range(j0, j0 + jn):
             y = jnp.dot(inner[b], wd[:, j * COLS:(j + 1) * COLS], preferred_element_type=f32)
             py[j, :, o0:o0 + on] = y.reshape(n_local, on, SUB, COLS).astype(bf16)
         js = pl.ds(j0, jn)
         send(py.at[js, pl.ds(other, nx), pl.ds(o0, on)], r1b.at[js, :, pl.ds(o0, on)],
-             ssem.at[3], c1.at[b, g], me_n, partner)
+             ssem.at[3], d1.at[b, g, 0], me_n, partner)
 
     def pair_sum(b, g):
         o0, on = batches[b]
-        j0, jn = cgroups[g]
+        j0, jn = groups[g]
         js, os = pl.ds(j0, jn), pl.ds(o0, on)
-        arrived(r1b.at[js, :, os], c1.at[b, g])
+        arrived(r1b.at[js, :, os], d1.at[b, g, 0])
         for d in range(1, nx):
             xd = x_at(d)
             for j in range(j0, j0 + jn):
                 s2[j, d - 1, o0:o0 + on] = (py[j, half + xd, o0:o0 + on].astype(f32)
                                             + r1b[j, xd, o0:o0 + on].astype(f32)).astype(bf16)
-            send(s2.at[js, d - 1, os], r2b.at[js, d - 1, os], ssem.at[4], c2.at[b, g], me_n, xd * 2 + me_c)
+            send(s2.at[js, d - 1, os], r2b.at[js, d - 1, os], ssem.at[4], d1.at[b, g, 1], me_n, xd * 2 + me_c)
 
     def answer(b, g):
         o0, on = batches[b]
-        j0, jn = cgroups[g]
+        j0, jn = groups[g]
         js, os = pl.ds(j0, jn), pl.ds(o0, on)
-        arrived(r2b.at[js, :, os], c2.at[b, g])
+        arrived(r2b.at[js, :, os], d1.at[b, g, 1])
         for j in range(j0, j0 + jn):
             total = py[j, mine, o0:o0 + on].astype(f32) + r1b[j, me_x, o0:o0 + on].astype(f32)
             for d in range(1, nx):
@@ -328,13 +326,16 @@
 
     run = {"pass_near": functools.partial(pass_part, far=False), "pass_far": functools.partial(pass_part, far=True), "pass_across": pass_across, "hidden": hidden, "down": down,
            "pair_sum": pair_sum, "answer": answer}
-    for name, b, g in plan([on for _, on in batches], len(dgroups), len(cgroups)):
+    for name, b, g in plan([on for _, on in batches], len(groups)):
         with jax.named_scope(f"{name}_{b}{g}"):
             run[name](b, g)
-    for g, (j0, jn) in enumerate(cgroups):
+        if (name, b, g) == ("pass_far", 0, len(groups) - 1):
+            for late in range(EARLY, len(batches)):
+                for i in range(len(groups)):
+                    send_out(late, i)
+    for g, (j0, jn) in enumerate(groups):
         with jax.named_scope(f"back_{g}"):
-            for b, (o0, on) in enumerate(batches):
-                arrived(ax.at[pl.ds(j0, jn), pl.ds(o0 * SUB, remote_rows(b))], c3.at[b, g])
+            arrived(ax.at[pl.ds(j0, jn), pl.ds(0, per - SLOT)], c3.at[g])
         for j in range(j0, j0 + jn):
             answers = from_tiles(ax[j], per, j % 2, 2)
             out_ref[:, j * COLS:(j + 1) * COLS] = jnp.dot(place, answers, preferred_element_type=f32).astype(bf16)
@@ -350,14 +351,14 @@
     nx = n_local // 2
     per = n_node * SLOT
     octs = per // SUB
-    nb, dg, cg = len(split(octs, BATCHES)), len(split(chunks, DISPATCH_GROUPS)), len(split(chunks, COMBINE_GROUPS))
+    nb, ng = len(batches_of(n_node)), len(split(chunks, GROUPS))
     deep = max(per, n_local * SUB * batches_of(n_node)[-1][1])
     bf16 = jnp.bfloat16
     vmem = pl.BlockSpec(memory_space=pltpu.VMEM)
     dma = pltpu.SemaphoreType.DMA
     buffers = [
         ((tok_dev, width), bf16),
-        ((width, 2 * ff), bf16),
+        ((2 * ff // LANE, width, LANE), bf16),
         ((ff, width), bf16),
         ((chunks, per, SUB, LANE), bf16),
         ((chunks, n_local, per, SUB, LANE), bf16),
@@ -381,9 +382,8 @@
             pltpu.VMEM(chosen.shape, chosen.dtype),
             pltpu.VMEM(gates.shape, gates.dtype),
             *(pltpu.VMEM(shape, kind) for shape, kind in buffers),
-            dma((6 + dg,)), dma((6,)),
-            dma((nb, dg, 2)), dma((nb, dg)), dma((nb, dg)),
-            dma((nb, cg)), dma((nb, cg)), dma((nb, cg)),
+            dma((4 + ng,)), dma((1,)), dma((6,)),
+            dma((nb, ng, 2)), dma((nb, ng)), dma((nb, ng)), dma((ng,)),
         ],
         compiler_params=pltpu.CompilerParams(
             collective_id=0, has_side_effects=True, vmem_limit_bytes=min(size + 14000000, 66000000)),

time: 34.4 us -> 33.3 us (0.968)
  Pallas kernels: 33 us -> 31.9 us
    pallas_call x1, Pallas kernels: 33 us -> 31.9 us  [shards(): pl.pallas_call(functools.partial(kernel, (n_node, n_local, chunks, tok_de...]
where the time goes in v3:
time: 33.3 us; the launch traced here: 33.2 us
  Pallas kernels  31.9 us (96%)
  local copies, waits for them, and re-layouts  1.23 us (4%)
    pallas_call x1, Pallas kernels, shards(): pl.pallas_call(functools.partial(kernel, (n_node, n_local, chunks, tok_de...  31.9 us
    unnamed x1, local copies, waits for them, and re-layouts  1.23 us

profile of v3, /device:TPU:0, one launch (start us, length us, event | category | flops | bytes accessed | tf_op | source)
XLA Modules:
  0.0 33.2 jit_solution(1295890399128281577)
XLA Ops:
  0.0 31.9 %shard_map.73 = bf16[128,7168]{1,0:T(8,128)(2,1)S(1)} custom-call(s32[8]{0:T(128)} %counts_hbm.1, s32[8,48]{1,0:T(8,128)} %chosen_hbm.1, f32[8,48]{1,0:T(8,128)} %gates_hbm.1, bf16[128,7168]{1,0:T(8,128)(2,1)} %tokens_hbm.1, bf16[1,7168,256]{2,1,0:T(8,128)(2,1)} %wg_hbm.1, bf16[1,7168,256]{2,1,0:T(8,128)(2,1)} %wu_hbm.1, bf16[1,256,7168]{2,1,0:T(8,128)(2,1)} %wd_hbm.1), custom_call_target="tpu_custom_call" | custom-call | tf_op jit(solution)/shard_map/pallas_call | solution.py:375
  32.0 1.2 %copy.9 = bf16[128,7168]{1,0:T(8,128)(2,1)} copy(bf16[128,7168]{1,0:T(8,128)(2,1)S(1)} %shard_map.73) | data formatting | bytes 3670016

commit v4 on v3

--- a/solution.py
+++ b/solution.py
@@ -56,7 +56,7 @@
     wire = [7.0 * size / total / ng for size in sizes]
     work = {"pass_near": 0.02, "pass_far": 0.02, "pass_across": 0.02, "pair_sum": 0.03, "answer": 0.05,
             "hidden": 1.65 / ng, "down": 1.0 / ng}
-    rank = {name: i for i, name in enumerate(("pass_far", "pass_near", "pass_across", "pair_sum", "answer", "hidden", "down"))}
+    rank = {name: i for i, name in enumerate(("pair_sum", "pass_far", "pass_near", "pass_across", "answer", "hidden", "down"))}
     ready = {}
     passed = 0.0
     for b in range(nb):

time: 33.3 us -> 33.4 us (level)
  no operation moved by 1% of the time
where the time goes in v4:
time: 33.4 us; the launch traced here: 33.2 us
  Pallas kernels  32 us (96%)
  local copies, waits for them, and re-layouts  1.23 us (4%)
    pallas_call x1, Pallas kernels, shards(): pl.pallas_call(functools.partial(kernel, (n_node, n_local, chunks, tok_de...  32 us
    unnamed x1, local copies, waits for them, and re-layouts  1.23 us

profile of v4, /device:TPU:0, one launch (start us, length us, event | category | flops | bytes accessed | tf_op | source)
XLA Modules:
  0.0 33.2 jit_solution(16499592613508821788)
XLA Ops:
  0.0 32.0 %shard_map.73 = bf16[128,7168]{1,0:T(8,128)(2,1)S(1)} custom-call(s32[8]{0:T(128)} %counts_hbm.1, s32[8,48]{1,0:T(8,128)} %chosen_hbm.1, f32[8,48]{1,0:T(8,128)} %gates_hbm.1, bf16[128,7168]{1,0:T(8,128)(2,1)} %tokens_hbm.1, bf16[1,7168,256]{2,1,0:T(8,128)(2,1)} %wg_hbm.1, bf16[1,7168,256]{2,1,0:T(8,128)(2,1)} %wu_hbm.1, bf16[1,256,7168]{2,1,0:T(8,128)(2,1)} %wd_hbm.1), custom_call_target="tpu_custom_call" | custom-call | tf_op jit(solution)/shard_map/pallas_call | solution.py:375
  32.0 1.2 %copy.9 = bf16[128,7168]{1,0:T(8,128)(2,1)} copy(bf16[128,7168]{1,0:T(8,128)(2,1)S(1)} %shard_map.73) | data formatting | bytes 3670016
